TPU v7x, 32 devices: a whole 2x2x4 slice. The times are simulated.
32 devices in a mesh: lev: 2 (over core), wa: 16 (over z, y, x).
Axes of the slice: x: 2, y: 2, z: 4, core: 2. Of those that a mesh axis runs over, the one named last changes fastest.
Arguments:
- spectral: bfloat16 [1280, 1280, 2, 64], P('wa', None, None, 'lev'), parts along dimension 3, may hold values from -0.15625 to 0.15625
- legendre: bfloat16 [1280, 1280, 48], P('wa'), may hold values from -0.15625 to 0.15625
- wavenumber: int32 [1280], P('wa'), may hold values from 0 to 1279, each once
Outputs:
- grid: float32 [96, 2560, 64], P('wa', None, 'lev'), parts along dimension 2
There are 2 independent parts, one for each index of `lev`. A program takes and returns all parts, laid end to end along the dimension named above; an argument that names none is the same for every part. Nothing has to cross between parts.
Inputs may be any that keep to these rules, and one draw needn't show every extreme that they name: wavenumber names every number of 0 to 1279 exactly once; slot k of spectral and legendre belongs to wavenumber[k].
All inputs are finite; a program needn't handle non-finite values.
Results may differ from a plain program's by a relative error of at most 0.0003.
Values sent between devices are 32-bit elements.
A program may use at most 128 MiB of HBM per device.

v0:
```python
import math

import jax
import jax.numpy as jnp
from jax import lax
from jax.sharding import PartitionSpec as P

NLON = 2560


def parity_columns(coeff_rows, offset):
    kept_rows = offset >= 0
    even_rows = jnp.logical_and(kept_rows, offset % 2 == 0)[..., None]
    odd_rows = jnp.logical_and(kept_rows, offset % 2 == 1)[..., None]
    nothing = jnp.zeros_like(coeff_rows)
    return jnp.concatenate(
        [jnp.where(even_rows, coeff_rows, nothing), jnp.where(odd_rows, coeff_rows, nothing)], -1
    )


def legendre_every(legendre, coeff_rows, wavenumber):
    row_index = jnp.arange(legendre.shape[1], dtype=jnp.int32)
    split_terms = parity_columns(coeff_rows, row_index[None, :] - wavenumber[:, None])
    return lax.dot_general(
        legendre, split_terms, (((1,), (1,)), ((0,), (0,))), preferred_element_type=jnp.float32
    )


def band_columns(legendre, coeff_rows, wavenumber):
    sums = legendre_every(legendre, coeff_rows, wavenumber)
    columns = coeff_rows.shape[-1]
    even_sums = sums[..., :columns]
    odd_sums = sums[..., columns:]
    return jnp.concatenate([even_sums + odd_sums, (even_sums - odd_sums)[:, ::-1]], 1)


def synthesis(fourier, slot_order, levels):
    longitude = jnp.arange(NLON, dtype=jnp.int32)
    phase_index = slot_order[:, None] * longitude[None, :] % NLON
    lon_angle = phase_index.astype(jnp.float32) * (2.0 * math.pi / NLON)
    weighting = jnp.where(slot_order == 0, 1.0, 2.0).astype(jnp.float32)[:, None]
    cos_sin = jnp.concatenate([weighting * jnp.cos(lon_angle), -weighting * jnp.sin(lon_angle)], 0)
    stacked = jnp.concatenate([fourier[..., :levels], fourier[..., levels:]], 0)
    gridded = lax.dot_general(
        stacked,
        cos_sin,
        (((0,), (0,)), ((), ())),
        precision=lax.Precision.HIGHEST,
        preferred_element_type=jnp.float32,
    )
    return jnp.transpose(gridded, (0, 2, 1))


def on_device(spectral, legendre, wavenumber):
    slot_count = spectral.shape[0]
    degrees = spectral.shape[1]
    levels = spectral.shape[3]
    coeff_rows = spectral.reshape(slot_count, degrees, 2 * levels)
    devices = lax.axis_size("wa")
    every_wave = lax.all_gather(wavenumber, "wa", axis=0, tiled=True)
    by_device = every_wave.reshape(devices, slot_count)
    middle = slot_count // 2
    pieces = []
    orders = []
    for low_slot, high_slot in ((0, middle), (middle, slot_count)):
        columns = band_columns(
            legendre[low_slot:high_slot],
            coeff_rows[low_slot:high_slot],
            wavenumber[low_slot:high_slot],
        )
        pieces.append(lax.all_to_all(columns, "wa", split_axis=1, concat_axis=0, tiled=True))
        orders.append(by_device[:, low_slot:high_slot].reshape(-1))
    fourier = jnp.concatenate(pieces, 0)
    slot_order = jnp.concatenate(orders, 0)
    return synthesis(fourier, slot_order, levels)


def solution(mesh):
    return jax.shard_map(
        on_device,
        mesh=mesh,
        in_specs=(P("wa", None, None, "lev"), P("wa", None, None), P("wa")),
        out_specs=P("wa", None, "lev"),
        check_vma=False,
    )
```

profile of v0, /device:TPU:0, one launch (start us, length us, event | category | flops | bytes accessed | tf_op | source)
XLA Modules:
  0.0 247.6 jit_solution(8109818152689006272)
XLA Ops:
  0.0 0.8 fusion.54
  0.8 9.7 %fusion.52 = (bf16[40,1280,2,32]{1,3,2,0:T(8,128)(2,1)}, bf16[40,1280,2,32]{1,3,2,0:T(8,128)(2,1)}) fusion(bf16[80,1280,2,32]{1,3,2,0:T(8,128)(2,1)} %param.3), kind=kLoop, calls=%fused_computation.72 | loop fusion | bytes 26214400 | tf_op jit(solution)/shard_map/slice | solution.py:68
  10.5 13.3 %copy.18 = bf16[40,1280,64]{2,1,0:T(8,128)(2,1)} copy(bf16[40,1280,64]{1,2,0:T(8,128)(2,1)} %bitcast.31) | data formatting | bytes 13107200 | tf_op jit(solution)/shard_map/slice | solution.py:68
  23.8 0.4 fusion.40
  24.2 21.0 %broadcast_select_fusion.3 = (bf16[40,1280,64]{2,1,0:T(8,128)(2,1)S(1)}, bf16[40,1280,64]{2,1,0:T(8,128)(2,1)}) fusion(bf16[40,1280,64]{2,1,0:T(8,128)(2,1)} %copy.18, pred[40,1280]{1,0:T(8,128)(4,1)S(1)} %get-tuple-element.28, pred[40,1280]{1,0:T(8,128)(4,1)S(1)} %get-tuple-element.27), kind=kLoop, calls=%fused_computation.24 | loop fusion | flops 6553600 | bytes 19763200 | tf_op jit(solution)/shard_map/jit(_where)/select_n | solution.py:17
  45.2 11.0 %fusion.28 = f32[40,48,128]{2,1,0:T(8,128)S(1)} fusion(bf16[40,1280,64]{2,1,0:T(8,128)(2,1)} %get-tuple-element.6, bf16[40,1280,64]{2,1,0:T(8,128)(2,1)S(1)} %get-tuple-element.5, bf16[80,1280,48]{1,2,0:T(8,128)(2,1)} %param.4), kind=kOutput, calls=%fused_computation.37 | convolution fusion | flops 655360000 | bytes 25559040 | tf_op jit(solution)/shard_map/dot_general | solution.py:24
  56.1 0.3 slice_add_fusion.1
  56.5 1.4 rev.6
  57.9 0.2 pad_maximum_fusion.1
  58.1 1.1 copy.31
  59.3 2.2 reshape.158
  61.4 8.4 %all-to-all-start = ((f32[16,1,15360]{2,1,0:T(1,128)}), f32[16,1,15360]{2,1,0:T(1,128)S(1)}, u32[]{:S(2)}, u32[]{:S(2)}) async-start(f32[16,1,15360]{2,1,0:T(1,128)} %reshape.158), calls=%async_computation | async-start | bytes 1966080 | tf_op jit(solution)/shard_map/all_to_all | solution.py:71
  69.9 13.3 %copy.22 = bf16[40,1280,64]{2,1,0:T(8,128)(2,1)} copy(bf16[40,1280,64]{1,2,0:T(8,128)(2,1)} %bitcast.30) | data formatting | bytes 13107200 | tf_op jit(solution)/shard_map/slice | solution.py:68
  83.2 21.0 %broadcast_select_fusion.1 = (bf16[40,1280,64]{2,1,0:T(8,128)(2,1)S(1)}, bf16[40,1280,64]{2,1,0:T(8,128)(2,1)}) fusion(bf16[40,1280,64]{2,1,0:T(8,128)(2,1)} %copy.22, pred[40,1280]{1,0:T(8,128)(4,1)S(1)} %get-tuple-element.25, pred[40,1280]{1,0:T(8,128)(4,1)S(1)} %get-tuple-element.26), kind=kLoop, calls=%fused_computation.22 | loop fusion | flops 6553600 | bytes 19763200 | tf_op jit(solution)/shard_map/jit(_where)/select_n | solution.py:17
  104.1 11.0 %fusion.23 = f32[40,48,128]{2,1,0:T(8,128)S(1)} fusion(bf16[40,1280,64]{2,1,0:T(8,128)(2,1)} %get-tuple-element.10, bf16[40,1280,64]{2,1,0:T(8,128)(2,1)S(1)} %get-tuple-element.9, bf16[80,1280,48]{1,2,0:T(8,128)(2,1)} %param.4), kind=kOutput, calls=%fused_computation.36 | convolution fusion | flops 655360000 | bytes 25559040 | tf_op jit(solution)/shard_map/dot_general | solution.py:24
  115.1 0.0 copy-start.1
  115.1 0.0 copy-start
  115.1 1.6 slice_add_fusion
  116.7 1.8 rev.7
  118.5 1.5 pad_maximum_fusion.2
  120.0 1.1 copy.30
  121.1 2.2 reshape.156
  123.3 0.0 copy-done.1
  123.3 0.6 dynamic-slice
  124.5 0.0 copy-done
  124.5 0.3 dynamic-update-slice
  124.8 15.1 %all-reduce = s32[1280]{0:T(1024)S(1)} all-reduce(s32[1280]{0:T(1024)S(1)} %dynamic-update-slice), channel_id=1, replica_groups=mesh['lev'=2,'wa'=16] {'wa'}, use_global_device_ids=true, to_apply=%add | all-reduce | flops 1280 | bytes 10240
  139.9 0.1 reshape.149
  139.9 0.1 fusion.53
  140.0 0.1 concatenate.41
  140.1 0.1 concatenate.42
  140.2 0.0 all-to-all-done
  140.2 4.5 %all-to-all-start.1 = ((f32[16,1,15360]{2,1,0:T(1,128)}), f32[16,1,15360]{2,1,0:T(1,128)}, u32[]{:S(2)}, u32[]{:S(2)}) async-start(f32[16,1,15360]{2,1,0:T(1,128)} %reshape.156), calls=%async_computation.1 | async-start | bytes 1966080 | tf_op jit(solution)/shard_map/all_to_all | solution.py:71
  144.8 57.7 %cosine_multiply_fusion = (f32[1280,2560]{1,0:T(8,128)}, f32[1280,2560]{1,0:T(8,128)}) fusion(s32[1280]{0:T(1024)S(1)} %constant_dynamic-update-slice_fusion, f32[1280]{0:T(1024)S(1)} %get-tuple-element.17, f32[1280]{0:T(1024)S(1)} %get-tuple-element.18), kind=kLoop, calls=%fused_computation.16 | loop fusion | flops 36044800 | bytes 26229760 | tf_op jit(solution)/shard_map/mul | solution.py:42
  202.5 0.6 broadcast.214
  203.0 4.2 %reduce.1 = f32[16,15360]{1,0:T(8,128)} reduce(f32[16,1,15360]{2,1,0:T(1,128)S(1)} %all-to-all-done, f32[]{:T(128)} %broadcast.214), dimensions={1}, to_apply=%all_to_all.26.reduce_sub_computation | reduce | bytes 1966084 | tf_op jit(solution)/shard_map/all_to_all | solution.py:71
  207.3 1.7 reshape.159
  209.0 1.4 copy.21
  210.4 2.1 copy.26
  212.5 0.0 all-to-all-done.1
  212.5 5.2 %reduce = f32[16,15360]{1,0:T(8,128)} reduce(f32[16,1,15360]{2,1,0:T(1,128)} %all-to-all-done.1, f32[]{:T(128)} %broadcast.214), dimensions={1}, to_apply=%all_to_all.30.reduce_sub_computation | reduce | bytes 1966084 | tf_op jit(solution)/shard_map/all_to_all | solution.py:71
  217.7 1.7 reshape.157
  219.4 1.4 copy.25
  220.8 2.1 copy.27
  222.9 0.1 fusion.33
  223.0 24.6 %fusion.18 = f32[6,2560,32]{1,2,0:T(8,128)} fusion(f32[1280,2560]{1,0:T(8,128)} %get-tuple-element.16, f32[1280,2560]{1,0:T(8,128)} %get-tuple-element.15, f32[640,6,64]{0,2,1:T(8,128)S(1)} %copy.27, f32[640,6,64]{0,2,1:T(8,128)S(1)} %copy.26, f32[1280,6,32]{0,2,1:T(8,128)S(1)} %fusion.33), kind=kOutput, calls=%fused_computation.27 | convolution fusion | flops 15107031040 | bytes 31129600 | tf_op jit(solution)/shard_map/dot_general | solution.py:44
  (5 shorter events, 0.0 us)
Async XLA Ops:
  61.4 78.8 %all-to-all-start = ((f32[16,1,15360]{2,1,0:T(1,128)}), f32[16,1,15360]{2,1,0:T(1,128)S(1)}, u32[]{:S(2)}, u32[]{:S(2)}) async-start(f32[16,1,15360]{2,1,0:T(1,128)} %reshape.158), calls=%async_computation | async-start | bytes 1966080 | tf_op jit(solution)/shard_map/all_to_all | solution.py:71
  115.1 8.2 %copy-start.1 = (u32[32]{0:T(128)S(1)}, u32[32]{0:T(128)}, u32[]{:S(2)}) copy-start(u32[32]{0:T(128)} %constant.50) | copy-start | bytes 388
  115.1 9.4 %copy-start = (s32[80]{0:T(128)S(1)}, s32[80]{0:T(128)}, u32[]{:S(2)}) copy-start(s32[80]{0:T(128)} %param.5) | copy-start | bytes 964
  140.2 72.3 %all-to-all-start.1 = ((f32[16,1,15360]{2,1,0:T(1,128)}), f32[16,1,15360]{2,1,0:T(1,128)}, u32[]{:S(2)}, u32[]{:S(2)}) async-start(f32[16,1,15360]{2,1,0:T(1,128)} %reshape.156), calls=%async_computation.1 | async-start | bytes 1966080 | tf_op jit(solution)/shard_map/all_to_all | solution.py:71
where the time goes:
time: 249 us; the launch traced here: 248 us
  other arithmetic  113 us (45%)
  local copies, waits for them, and re-layouts  59.1 us (24%)
  matrix products  46.6 us (19%)
  blocking collectives  15.1 us (6%)
  starting transfers between devices  12.9 us (5%)
    mul x1, other arithmetic, synthesis(): weighting * jnp.cos(lon_angle)  57.7 us
    select_n x2, other arithmetic, parity_columns(): jnp.where(even_rows, coeff_rows, nothing)  41.9 us
    slice x3, local copies, waits for them, and re-layouts, on_device(): coeff_rows[low_slot:high_slot]  36.3 us
    dot_general x1, matrix products, synthesis(): lax.dot_general(stacked, cos_sin, (((0,), (0,)), ((), ())), precision=lax...  24.6 us
    dot_general x2, matrix products, legendre_every(): lax.dot_general(legendre, split_terms, (((1,), (1,)), ((0,), (0,))), pref...  22 us
    unnamed x1, blocking collectives  15.1 us
    all_to_all x2, starting transfers between devices, on_device(): lax.all_to_all(columns, 'wa', split_axis=1, concat_axis=0, tiled=True)  12.9 us
    all_to_all x2, other arithmetic, on_device(): lax.all_to_all(columns, 'wa', split_axis=1, concat_axis=0, tiled=True)  9.38 us
  transfers between devices with their start and end apart: 2, of which 0 were waited for; matrix products, arithmetic and copies ran while one was open for 49% of the time, Pallas kernels for 0%

commit v1 on v0

v1 whole, which is shorter than its diff:
```python
import functools
import math

import jax
import jax.numpy as jnp
from jax import lax
from jax.experimental import pallas as pl
from jax.experimental.pallas import tpu as pltpu
from jax.sharding import PartitionSpec as P

NLON = 2560
PAIRS = 8
TILE = 256


def exchange_kernel(
    n, chunks, real_pairs, north,
    wave_smem, wave_row, spectral, legendre,
    recv, wave_all,
    send, send_sem, recv_sem, wave_send, wave_recv, own_sem,
):
    me = lax.axis_index("wa")
    step = pl.program_id(0)
    half = n // 2
    block = 2 * north // n * PAIRS

    def rows_for(dst):
        south = dst // half
        slab = (1 - south) * dst + south * (half + n - 1 - dst)
        return pl.ds(pl.multiple_of(slab * block, 8), block)

    def wave_copy(i):
        dst = lax.rem(me + i, n)
        return pltpu.make_async_remote_copy(
            src_ref=wave_row, dst_ref=wave_all.at[me],
            send_sem=wave_send.at[dst], recv_sem=wave_recv.at[me],
            device_id={"wa": dst}, device_id_type=pl.DeviceIdType.MESH,
        )

    def data_copy(c, i):
        dst = lax.rem(me + i, n)
        return pltpu.make_async_remote_copy(
            src_ref=send.at[c, rows_for(dst)], dst_ref=recv.at[c, me],
            send_sem=send_sem.at[c, dst], recv_sem=recv_sem.at[c, me],
            device_id={"wa": dst}, device_id_type=pl.DeviceIdType.MESH,
        )

    def data_arrival(c, i):
        src = lax.rem(me + i, n)
        return pltpu.make_async_remote_copy(
            src_ref=send.at[c, rows_for(src)], dst_ref=recv.at[c, src],
            send_sem=send_sem.at[c, src], recv_sem=recv_sem.at[c, src],
            device_id={"wa": src}, device_id_type=pl.DeviceIdType.MESH,
        )

    def wave_arrival(i):
        src = lax.rem(me + i, n)
        return pltpu.make_async_remote_copy(
            src_ref=wave_row, dst_ref=wave_all.at[src],
            send_sem=wave_send.at[src], recv_sem=wave_recv.at[src],
            device_id={"wa": src}, device_id_type=pl.DeviceIdType.MESH,
        )

    def own_copy(c):
        return pltpu.make_async_copy(send.at[c, rows_for(me)], recv.at[c, me], own_sem.at[c])

    own_wave = pltpu.make_async_copy(wave_row, wave_all.at[me], own_sem.at[chunks])

    @pl.when(step == 0)
    def _():
        barrier = pltpu.get_barrier_semaphore()

        def greet(i, carry):
            pl.semaphore_signal(
                barrier, inc=1, device_id={"wa": lax.rem(me + i, n)},
                device_id_type=pl.DeviceIdType.MESH,
            )
            return carry

        lax.fori_loop(1, n, greet, 0)
        pl.semaphore_wait(barrier, n - 1)

        def send_wave(i, carry):
            wave_copy(i).start()
            return carry

        lax.fori_loop(1, n, send_wave, 0)
        own_wave.start()

    degrees = spectral.shape[-1]
    columns = spectral.shape[1]
    index = lax.broadcasted_iota(jnp.int32, (1, degrees), 1)
    lane = lax.broadcasted_iota(jnp.int32, (1, 2 * columns), 1)

    def sums_of(slot):
        offset = index - wave_smem[step * 2 * real_pairs + slot]
        keep = jnp.where(offset >= 0, 1.0, 0.0)
        flip = jnp.where(offset % 2 == 0, keep, -keep)
        coeff = spectral[slot]
        both = jnp.concatenate(
            [coeff * keep.astype(coeff.dtype), coeff * flip.astype(coeff.dtype)], 0
        )
        return lax.dot_general(
            legendre[slot], both, (((1,), (1,)), ((), ())), preferred_element_type=jnp.float32
        )

    for p in range(PAIRS):
        if p < real_pairs:
            first = sums_of(2 * p)
            second = sums_of(2 * p + 1)
            first_turned = pltpu.roll(first, columns, 1)
            second_turned = pltpu.roll(second, columns, 1)
            north_rows = jnp.where(lane < columns, first, second_turned)
            south_rows = jnp.where(lane < columns, first_turned, second)
        else:
            north_rows = south_rows = jnp.zeros((north, 2 * columns), jnp.float32)
        send[step, pl.ds(p, north, stride=PAIRS), :] = north_rows
        send[step, pl.ds(north * PAIRS + p, north, stride=PAIRS), :] = south_rows

    def send_data(i, carry):
        data_copy(step, i).start()
        return carry

    lax.fori_loop(1, n, send_data, 0)
    own_copy(step).start()

    @pl.when(step == chunks - 1)
    def _():
        own_wave.wait()

        def finish_wave(i, carry):
            wave_copy(i).wait_send()
            wave_arrival(i).wait_recv()
            return carry

        lax.fori_loop(1, n, finish_wave, 0)
        for c in range(chunks):
            own_copy(c).wait()

            def finish(i, carry, c=c):
                data_copy(c, i).wait_send()
                data_arrival(c, i).wait_recv()
                return carry

            lax.fori_loop(1, n, finish, 0)


def cos_sin(turns):
    quarter = jnp.floor(turns * (4.0 / NLON) + 0.5)
    x = (turns - quarter * (NLON // 4)) * (2.0 * math.pi / NLON)
    y = x * x
    s = x * (1.0 + y * (-1 / 6 + y * (1 / 120 + y * (-1 / 5040 + y * (1 / 362880)))))
    c = 1.0 + y * (-1 / 2 + y * (1 / 24 + y * (-1 / 720 + y * (1 / 40320 - y * (1 / 3628800)))))
    which = quarter.astype(jnp.int32) & 3
    odd = (which & 1) == 1
    cos_out = jnp.where(odd, s, c)
    sin_out = jnp.where(odd, c, s)
    cos_out = jnp.where((which == 1) | (which == 2), -cos_out, cos_out)
    sin_out = jnp.where(which >= 2, -sin_out, sin_out)
    return cos_out, sin_out


def synthesis_kernel(south_ref, wave_ref, data, out, hi, lo, cos_now, sin_now, table_hi, table_lo):
    step = pl.program_id(0)
    groups, rows, pairs, lanes = data.shape
    depth = groups * pairs
    levels = lanes // 4

    @pl.when(step == 0)
    def _():
        lane = lax.broadcasted_iota(jnp.int32, (1, lanes), 1)
        sign = jnp.where((lane // levels) % 2 == 1, -1.0, 1.0)
        weight = jnp.where(wave_ref[...] == 0.0, 1.0, 2.0)
        scale = jnp.where(lane < 2 * levels, weight[:depth], weight[depth:]) * sign
        south = south_ref[0]
        for row in range(rows):
            source = row + south * (rows - 1 - 2 * row)
            values = data[:, source].reshape(depth, lanes) * scale
            turned = values.T
            for g in range(4):
                part = turned[g * levels:(g + 1) * levels]
                part_hi = part.astype(jnp.bfloat16)
                place = (slice(row * levels, (row + 1) * levels), slice(g * depth, (g + 1) * depth))
                hi[place] = part_hi
                lo[place] = (part - part_hi.astype(jnp.float32)).astype(jnp.bfloat16)
        position = lax.broadcasted_iota(jnp.int32, (1, TILE), 1).astype(jnp.float32)

        def begin(i, carry):
            at = pl.ds(pl.multiple_of(i * 16, 16), 16)
            c, s = cos_sin(wave_ref[at, :] * position)
            cos_now[at, :] = c
            sin_now[at, :] = s
            return carry

        lax.fori_loop(0, 2 * depth // 16, begin, 0, unroll=2)

    for sp in range(2):
        def fill(i, carry, sp=sp):
            at = pl.ds(pl.multiple_of(sp * depth + i * 16, 16), 16)
            c = cos_now[at, :]
            s = sin_now[at, :]
            turn_c, turn_s = cos_sin(wave_ref[at, :] * float(TILE))
            for values, part in ((c, 0), (s, 1)):
                to = pl.ds(pl.multiple_of((2 * sp + part) * depth + i * 16, 16), 16)
                top = values.astype(jnp.bfloat16)
                table_hi[to, :] = top
                table_lo[to, :] = (values - top.astype(jnp.float32)).astype(jnp.bfloat16)
            cos_now[at, :] = c * turn_c - s * turn_s
            sin_now[at, :] = s * turn_c + c * turn_s
            return carry

        lax.fori_loop(0, depth // 16, fill, 0, unroll=4)
    high = table_hi[...]
    total = jnp.dot(hi[...], high, preferred_element_type=jnp.float32)
    total += jnp.dot(lo[...], high, preferred_element_type=jnp.float32)
    total += jnp.dot(hi[...], table_lo[...], preferred_element_type=jnp.float32)
    out[...] = total.reshape(out.shape)


def on_device(spectral, legendre, wavenumber):
    slots, degrees, _, levels = spectral.shape
    north = legendre.shape[2]
    n = lax.axis_size("wa")
    rows = 2 * north // n
    pairs = slots // 2
    real_pairs = min(pairs, PAIRS)
    chunks = pairs // real_pairs
    coeff = jnp.transpose(spectral, (0, 2, 3, 1)).reshape(slots, 2 * levels, degrees)
    values = jnp.transpose(legendre, (0, 2, 1))
    wave_row = jnp.broadcast_to(jnp.pad(wavenumber, (0, 128 - slots))[None], (8, 128))
    block = rows * PAIRS
    per_step = 2 * real_pairs
    recv, wave_all = pl.pallas_call(
        functools.partial(exchange_kernel, n, chunks, real_pairs, north),
        grid=(chunks,),
        out_shape=(
            jax.ShapeDtypeStruct((chunks, n, block, 4 * levels), jnp.float32),
            jax.ShapeDtypeStruct((n, 8, 128), jnp.int32),
        ),
        in_specs=[
            pl.BlockSpec(memory_space=pltpu.SMEM),
            pl.BlockSpec(memory_space=pltpu.VMEM),
            pl.BlockSpec((per_step, 2 * levels, degrees), lambda i: (i, 0, 0)),
            pl.BlockSpec((per_step, north, degrees), lambda i: (i, 0, 0)),
        ],
        out_specs=(pl.BlockSpec(memory_space=pl.ANY), pl.BlockSpec(memory_space=pl.ANY)),
        scratch_shapes=[
            pltpu.VMEM((chunks, 2 * north * PAIRS, 4 * levels), jnp.float32),
            pltpu.SemaphoreType.DMA((chunks, n)),
            pltpu.SemaphoreType.DMA((chunks, n)),
            pltpu.SemaphoreType.DMA((n,)),
            pltpu.SemaphoreType.DMA((n,)),
            pltpu.SemaphoreType.DMA((chunks + 1,)),
        ],
        compiler_params=pltpu.CompilerParams(
            collective_id=0, has_side_effects=True, dimension_semantics=("arbitrary",)
        ),
    )(wavenumber, wave_row, coeff, values)
    waves = wave_all[:, 0, :slots].reshape(n, chunks, real_pairs, 2)
    waves = jnp.pad(waves, ((0, 0), (0, 0), (0, PAIRS - real_pairs), (0, 0)))
    depth = chunks * n * PAIRS
    waves = jnp.transpose(waves, (3, 1, 0, 2)).reshape(2 * depth, 1).astype(jnp.float32)
    south = (lax.axis_index("wa") >= n // 2).astype(jnp.int32).reshape(1)
    grid = pl.pallas_call(
        synthesis_kernel,
        grid=(NLON // TILE,),
        out_shape=jax.ShapeDtypeStruct((rows, levels, NLON), jnp.float32),
        in_specs=[
            pl.BlockSpec(memory_space=pltpu.SMEM),
            pl.BlockSpec((2 * depth, 1), lambda i: (0, 0)),
            pl.BlockSpec((chunks * n, rows, PAIRS, 4 * levels), lambda i: (0, 0, 0, 0)),
        ],
        out_specs=pl.BlockSpec((rows, levels, TILE), lambda i: (0, 0, i)),
        scratch_shapes=[
            pltpu.VMEM((rows * levels, 4 * depth), jnp.bfloat16),
            pltpu.VMEM((rows * levels, 4 * depth), jnp.bfloat16),
            pltpu.VMEM((2 * depth, TILE), jnp.float32),
            pltpu.VMEM((2 * depth, TILE), jnp.float32),
            pltpu.VMEM((4 * depth, TILE), jnp.bfloat16),
            pltpu.VMEM((4 * depth, TILE), jnp.bfloat16),
        ],
        compiler_params=pltpu.CompilerParams(dimension_semantics=("arbitrary",)),
    )(south, waves, recv.reshape(chunks * n, rows, PAIRS, 4 * levels))
    return jnp.transpose(grid, (0, 2, 1))


def solution(mesh):
    return jax.shard_map(
        on_device,
        mesh=mesh,
        in_specs=(P("wa", None, None, "lev"), P("wa", None, None), P("wa")),
        out_specs=P("wa", None, "lev"),
        check_vma=False,
    )
```

time: 249 us -> 102 us (0.41)
  other arithmetic: 113 us -> 0.85 us
  Pallas kernels: 0 us -> 97.2 us
  local copies, waits for them, and re-layouts: 59.1 us -> 2.49 us
  matrix products: 46.6 us -> 0 us
  blocking collectives: 15.1 us -> 0 us
  starting transfers between devices: 12.9 us -> 0 us
    pallas_call x0 -> x2, Pallas kernels: none -> 97.2 us  [the longest x1 53.9 us: on_device(): pl.pallas_call(functools.partial(exchange_kernel, n, chunks, real_pairs,...]
    mul x1 -> x0, other arithmetic: 57.7 us -> none  [synthesis(): weighting * jnp.cos(lon_angle)]
    dot_general x3 -> x0, matrix products: 46.6 us -> none  [the longest x1 24.6 us: synthesis(): lax.dot_general(stacked, cos_sin, (((0,), (0,)), ((), ())), precision=lax...]
    select_n x3 -> x0, other arithmetic: 41.9 us -> none  [the longest x2 41.9 us: parity_columns(): jnp.where(even_rows, coeff_rows, nothing)]
    slice x5 -> x0, local copies, waits for them, and re-layouts: 37.2 us -> none  [the longest x3 36.3 us: on_device(): coeff_rows[low_slot:high_slot]]
    unnamed x1 -> x0, blocking collectives: 15.1 us -> none
    all_to_all x2 -> x0, starting transfers between devices: 12.9 us -> none  [on_device(): lax.all_to_all(columns, 'wa', split_axis=1, concat_axis=0, tiled=True)]
    all_to_all x2 -> x0, other arithmetic: 9.38 us -> none  [on_device(): lax.all_to_all(columns, 'wa', split_axis=1, concat_axis=0, tiled=True)]
  transfers between devices with their start and end apart: 2 -> 0, of which waited for: 0 -> 0; matrix products, arithmetic and copies ran while one was open for 49% -> 0% of each run, Pallas kernels for 0% -> 0%
where the time goes in v1:
time: 102 us; the launch traced here: 101 us
  Pallas kernels  97.2 us (95%)
  local copies, waits for them, and re-layouts  2.49 us (2%)
    pallas_call x1, Pallas kernels, on_device(): pl.pallas_call(functools.partial(exchange_kernel, n, chunks, real_pairs,...  53.9 us
    pallas_call x1, Pallas kernels, on_device(): pl.pallas_call(synthesis_kernel, grid=(NLON // TILE,), out_shape=jax.Shap...  43.4 us

profile of v1, /device:TPU:0, one launch (start us, length us, event | category | flops | bytes accessed | tf_op | source)
XLA Modules:
  0.0 100.6 jit_solution(17041246141962562323)
XLA Ops:
  0.0 0.7 pad.4
  0.7 0.6 broadcast_in_dim.2.wave_row
  1.3 53.9 %shard_map.37 = (f32[5,16,48,128]{3,2,1,0:T(8,128)}, s32[16,8,128]{2,1,0:T(8,128)}) custom-call(s32[80]{0:T(128)} %wave_smem.1, s32[8,128]{1,0:T(8,128)} %broadcast_in_dim.2.wave_row, bf16[80,64,1280]{2,1,0:T(8,128)(2,1)} %bitcast.12, bf16[80,48,1280]{2,1,0:T(8,128)(2,1)} %bitcast.13), custom_call_target="tpu_custom_call" | custom-call | tf_op jit(solution)/shard_map/pallas_call | solution.py:233
  55.1 0.8 slice_convert_fusion
  56.0 0.1 copy.8
  56.1 0.1 copy.9
  56.2 1.1 %convert_element_type.14.wave_ref = f32[1280,1]{1,0:T(8,128)} reshape(f32[2,5,16,8]{3,2,1,0:T(8,128)S(1)} %copy.9) | data formatting | bytes 10240 | tf_op jit(solution)/shard_map/convert_element_type | solution.py:262
  57.2 43.4 %shard_map.38 = f32[6,32,2560]{2,1,0:T(8,128)} custom-call(s32[1]{0:T(128)} %bitcast.south_ref, f32[1280,1]{1,0:T(8,128)} %convert_element_type.14.wave_ref, f32[80,6,8,128]{3,2,1,0:T(8,128)} %bitcast.14), custom_call_target="tpu_custom_call" | custom-call | tf_op jit(solution)/shard_map/pallas_call | solution.py:264

commit v2 on v0

v2 whole, which is shorter than its diff:
```python
import functools
import math

import jax
import jax.numpy as jnp
from jax import lax
from jax.experimental import pallas as pl
from jax.experimental.pallas import tpu as pltpu
from jax.sharding import PartitionSpec as P

NLON = 2560
PAIRS = 8
TILE = 256
LANES = 128


def cos_sin(turns):
    quarter = jnp.floor(turns * (4.0 / NLON) + 0.5)
    x = (turns - quarter * (NLON // 4)) * (2.0 * math.pi / NLON)
    y = x * x
    s = x * (1.0 + y * (-1 / 6 + y * (1 / 120 + y * (-1 / 5040 + y * (1 / 362880)))))
    c = 1.0 + y * (-1 / 2 + y * (1 / 24 + y * (-1 / 720 + y * (1 / 40320 - y * (1 / 3628800)))))
    which = quarter.astype(jnp.int32) & 3
    odd = (which & 1) == 1
    cos_out = jnp.where(odd, s, c)
    sin_out = jnp.where(odd, c, s)
    cos_out = jnp.where((which == 1) | (which == 2), -cos_out, cos_out)
    sin_out = jnp.where(which >= 2, -sin_out, sin_out)
    return cos_out, sin_out


def transform_kernel(
    n, chunks, real_pairs, north,
    wave_smem, spectral, legendre,
    out,
    send, recv, wave_row, wave_all, wave_columns, wave_rows,
    cos_hi, cos_lo, sin_hi, sin_lo, even, odd,
    send_sem, recv_sem, wave_send, wave_recv, own_sem,
):
    me = lax.axis_index("wa")
    step = pl.program_id(0)
    half = n // 2
    rows = 2 * north // n
    block = rows * PAIRS

    def rows_for(dst):
        south = dst // half
        slab = (1 - south) * dst + south * (half + n - 1 - dst)
        return pl.ds(pl.multiple_of(slab * block, 8), block)

    def wave_copy(peer, owner):
        return pltpu.make_async_remote_copy(
            src_ref=wave_row, dst_ref=wave_all.at[owner],
            send_sem=wave_send.at[peer], recv_sem=wave_recv.at[owner],
            device_id={"wa": peer}, device_id_type=pl.DeviceIdType.MESH,
        )

    def data_copy(c, peer, owner):
        return pltpu.make_async_remote_copy(
            src_ref=send.at[c, rows_for(peer)], dst_ref=recv.at[c, owner],
            send_sem=send_sem.at[c, peer], recv_sem=recv_sem.at[c, owner],
            device_id={"wa": peer}, device_id_type=pl.DeviceIdType.MESH,
        )

    def own_copy(c):
        return pltpu.make_async_copy(send.at[c, rows_for(me)], recv.at[c, me], own_sem.at[c])

    own_wave = pltpu.make_async_copy(wave_row, wave_all.at[me], own_sem.at[chunks])

    def each_peer(act):
        def one(i, carry):
            act(lax.rem(me + i, n))
            return carry

        lax.fori_loop(1, n, one, 0)

    @pl.when(step == 0)
    def _():
        barrier = pltpu.get_barrier_semaphore()
        each_peer(
            lambda peer: pl.semaphore_signal(
                barrier, inc=1, device_id={"wa": peer}, device_id_type=pl.DeviceIdType.MESH
            )
        )
        place = lax.broadcasted_iota(jnp.int32, wave_row.shape, 1)
        waves = jnp.zeros(wave_row.shape, jnp.int32)
        for slot in range(wave_smem.shape[0]):
            waves = jnp.where(place == slot, wave_smem[slot], waves)
        wave_row[...] = waves
        pl.semaphore_wait(barrier, n - 1)
        each_peer(lambda peer: wave_copy(peer, me).start())
        own_wave.start()

    degrees = spectral.shape[-1]
    columns = spectral.shape[1]
    levels = columns // 2
    index = lax.broadcasted_iota(jnp.int32, (1, degrees), 1)
    lane = lax.broadcasted_iota(jnp.int32, (1, 2 * columns), 1)

    def sums_of(slot):
        offset = index - wave_smem[step * 2 * real_pairs + slot]
        keep = jnp.where(offset >= 0, 1.0, 0.0)
        flip = jnp.where(offset % 2 == 0, keep, -keep)
        coeff = spectral[slot]
        both = jnp.concatenate(
            [coeff * keep.astype(coeff.dtype), coeff * flip.astype(coeff.dtype)], 0
        )
        return lax.dot_general(
            legendre[slot], both, (((1,), (1,)), ((), ())), preferred_element_type=jnp.float32
        )

    for p in range(PAIRS):
        if p < real_pairs:
            first = sums_of(2 * p)
            second = sums_of(2 * p + 1)
            first_turned = pltpu.roll(first, columns, 1)
            second_turned = pltpu.roll(second, columns, 1)
            north_rows = jnp.where(lane < columns, first, second_turned)
            south_rows = jnp.where(lane < columns, first_turned, second)
        else:
            north_rows = south_rows = jnp.zeros((north, 2 * columns), jnp.float32)
        send[step, pl.ds(p, north, stride=PAIRS), :] = north_rows
        send[step, pl.ds(north * PAIRS + p, north, stride=PAIRS), :] = south_rows

    each_peer(lambda peer: data_copy(step, peer, me).start())
    own_copy(step).start()

    @pl.when(step == chunks - 1)
    def _():
        own_wave.wait()
        each_peer(lambda peer: wave_copy(peer, peer).wait_recv())
        gathered = wave_all[:, 0, :].astype(jnp.float32)
        if n < LANES:
            gathered = jnp.concatenate([gathered, jnp.zeros((LANES - n, LANES), jnp.float32)], 0)
        wave_columns[...] = gathered.T
        for c in range(chunks):
            for sp in range(2):
                own = wave_columns[pl.ds(c * 2 * real_pairs + sp, PAIRS, stride=2), :]
                for owner in range(n):
                    to = ((2 * c + sp) * n + owner) * PAIRS
                    wave_rows[to:to + PAIRS, :] = jnp.broadcast_to(
                        own[:, owner:owner + 1], (PAIRS, LANES)
                    )
        position = lax.broadcasted_iota(jnp.int32, (1, LANES), 1).astype(jnp.float32)
        sin_tiles = sin_hi.shape[1] // LANES

        def fill(i, carry):
            at = pl.ds(pl.multiple_of(i * 16, 16), 16)
            waves = wave_rows[at, :]
            weight = jnp.where(waves == 0.0, 1.0, 2.0)
            c, s = cos_sin(waves * position)
            turn_c, turn_s = cos_sin(waves * float(LANES))
            c, s = c * weight, s * weight
            for tile in range(sin_tiles + 1):
                to = slice(tile * LANES, (tile + 1) * LANES)
                top = c.astype(jnp.bfloat16)
                cos_hi[at, to] = top
                cos_lo[at, to] = (c - top.astype(jnp.float32)).astype(jnp.bfloat16)
                if tile < sin_tiles:
                    top = s.astype(jnp.bfloat16)
                    sin_hi[at, to] = top
                    sin_lo[at, to] = (s - top.astype(jnp.float32)).astype(jnp.bfloat16)
                    c, s = c * turn_c - s * turn_s, s * turn_c + c * turn_s
            return carry

        lax.fori_loop(0, wave_rows.shape[0] // 16, fill, 0)
        south = me // half
        depth = n * PAIRS

        def add_chunk(c, first):
            own_copy(c).wait()
            each_peer(lambda peer: data_copy(c, peer, peer).wait_recv())
            parts = [[], []]
            for row in range(rows):
                source = row + south * (rows - 1 - 2 * row)
                at = pl.ds(pl.multiple_of(source * PAIRS, 8), PAIRS)
                turned = recv[c, :, at, :].reshape(depth, 4 * levels).T
                for part in range(2):
                    parts[part].append(
                        jnp.concatenate(
                            [turned[part * levels:(part + 1) * levels],
                             turned[(2 + part) * levels:(3 + part) * levels]], 1
                        )
                    )
            at = pl.ds(pl.multiple_of(c * 2 * depth, 16), 2 * depth)
            for part, total, high, low in ((0, even, cos_hi, cos_lo), (1, odd, sin_hi, sin_lo)):
                values = jnp.concatenate(parts[part], 0)
                top = values.astype(jnp.bfloat16)
                rest = (values - top.astype(jnp.float32)).astype(jnp.bfloat16)
                table = high[at, :]
                sums = jnp.dot(top, table, preferred_element_type=jnp.float32)
                sums += jnp.dot(rest, table, preferred_element_type=jnp.float32)
                sums += jnp.dot(top, low[at, :], preferred_element_type=jnp.float32)
                if first:
                    total[...] = sums
                else:
                    total[...] += sums

        add_chunk(0, True)
        if chunks > 1:
            def later(c, carry):
                add_chunk(c, False)
                return carry

            lax.fori_loop(1, chunks, later, 0)

        r = lax.broadcasted_iota(jnp.int32, (TILE, TILE), 0)
        x = lax.broadcasted_iota(jnp.int32, (TILE, TILE), 1)
        mirror = jnp.where(r + x == TILE, 1.0, 0.0).astype(jnp.bfloat16)
        at_zero = lax.broadcasted_iota(jnp.int32, (1, TILE), 1) == 0
        tiles = odd.shape[1] // TILE
        after = even[:, tiles * TILE:tiles * TILE + 1]
        for tile in range(tiles - 1, -1, -1):
            to = slice(tile * TILE, (tile + 1) * TILE)
            back = slice((2 * tiles - 1 - tile) * TILE, (2 * tiles - tile) * TILE)
            e, o = even[:, to], odd[:, to]
            out[:, :, to] = (e - o).reshape(rows, levels, TILE)
            d = e + o
            top = d.astype(jnp.bfloat16)
            rest = (d - top.astype(jnp.float32)).astype(jnp.bfloat16)
            turned = jnp.dot(top, mirror, preferred_element_type=jnp.float32)
            turned += jnp.dot(rest, mirror, preferred_element_type=jnp.float32)
            out[:, :, back] = jnp.where(at_zero, after, turned).reshape(rows, levels, TILE)
            after = d[:, 0:1]
        each_peer(lambda peer: wave_copy(peer, me).wait_send())
        for c in range(chunks):
            each_peer(lambda peer, c=c: data_copy(c, peer, me).wait_send())


def on_device(spectral, legendre, wavenumber):
    slots, degrees, _, levels = spectral.shape
    north = legendre.shape[2]
    n = lax.axis_size("wa")
    rows = 2 * north // n
    pairs = slots // 2
    real_pairs = min(pairs, PAIRS)
    chunks = pairs // real_pairs
    coeff = jnp.transpose(spectral, (0, 2, 3, 1)).reshape(slots, 2 * levels, degrees)
    values = jnp.transpose(legendre, (0, 2, 1))
    block = rows * PAIRS
    per_step = 2 * real_pairs
    depth = 2 * chunks * n * PAIRS
    middle = NLON // 2
    grid = pl.pallas_call(
        functools.partial(transform_kernel, n, chunks, real_pairs, north),
        grid=(chunks,),
        out_shape=jax.ShapeDtypeStruct((rows, levels, NLON), jnp.float32),
        in_specs=[
            pl.BlockSpec(memory_space=pltpu.SMEM),
            pl.BlockSpec((per_step, 2 * levels, degrees), lambda i: (i, 0, 0)),
            pl.BlockSpec((per_step, north, degrees), lambda i: (i, 0, 0)),
        ],
        out_specs=pl.BlockSpec(memory_space=pltpu.VMEM),
        scratch_shapes=[
            pltpu.VMEM((chunks, 2 * north * PAIRS, 4 * levels), jnp.float32),
            pltpu.VMEM((chunks, n, block, 4 * levels), jnp.float32),
            pltpu.VMEM((8, LANES), jnp.int32),
            pltpu.VMEM((n, 8, LANES), jnp.int32),
            pltpu.VMEM((LANES, LANES), jnp.float32),
            pltpu.VMEM((depth, LANES), jnp.float32),
            pltpu.VMEM((depth, middle + LANES), jnp.bfloat16),
            pltpu.VMEM((depth, middle + LANES), jnp.bfloat16),
            pltpu.VMEM((depth, middle), jnp.bfloat16),
            pltpu.VMEM((depth, middle), jnp.bfloat16),
            pltpu.VMEM((rows * levels, middle + LANES), jnp.float32),
            pltpu.VMEM((rows * levels, middle), jnp.float32),
            pltpu.SemaphoreType.DMA((chunks, n)),
            pltpu.SemaphoreType.DMA((chunks, n)),
            pltpu.SemaphoreType.DMA((n,)),
            pltpu.SemaphoreType.DMA((n,)),
            pltpu.SemaphoreType.DMA((chunks + 1,)),
        ],
        compiler_params=pltpu.CompilerParams(
            collective_id=0, has_side_effects=True, dimension_semantics=("arbitrary",)
        ),
    )(wavenumber, coeff, values)
    return jnp.transpose(grid, (0, 2, 1))


def solution(mesh):
    return jax.shard_map(
        on_device,
        mesh=mesh,
        in_specs=(P("wa", None, None, "lev"), P("wa", None, None), P("wa")),
        out_specs=P("wa", None, "lev"),
        check_vma=False,
    )
```

time: 249 us -> 62.1 us (0.25)
  the two profiles are of different devices: /device:TPU:0 before, /device:TPU:15 now
where the time goes in v2:
time: 62.1 us; the launch traced here: 61.9 us
  Pallas kernels  58.9 us (95%)
  local copies, waits for them, and re-layouts  2.99 us (5%)
    pallas_call x1, Pallas kernels, on_device(): pl.pallas_call(functools.partial(transform_kernel, n, chunks, real_pairs,...  58.9 us
    unnamed x1, local copies, waits for them, and re-layouts  2.99 us

profile of v2, /device:TPU:15, one launch (start us, length us, event | category | flops | bytes accessed | tf_op | source)
XLA Modules:
  0.0 61.9 jit_solution(17117856911372376459)
XLA Ops:
  0.0 58.9 %shard_map.37 = f32[6,32,2560]{2,1,0:T(8,128)} custom-call(s32[80]{0:T(128)} %wave_smem.1, bf16[80,64,1280]{2,1,0:T(8,128)(2,1)} %bitcast.5, bf16[80,48,1280]{2,1,0:T(8,128)(2,1)} %bitcast.6), custom_call_target="tpu_custom_call" | custom-call | tf_op jit(solution)/shard_map/pallas_call | solution.py:244
  58.9 3.0 %copy.5 = f32[6,2560,32]{1,2,0:T(8,128)} copy(f32[6,2560,32]{1,2,0:T(8,128)} %bitcast.7) | data formatting | bytes 3932160

commit v3 on v2

--- a/solution.py
+++ b/solution.py
@@ -68,11 +68,18 @@
     own_wave = pltpu.make_async_copy(wave_row, wave_all.at[me], own_sem.at[chunks])
 
     def each_peer(act):
-        def one(i, carry):
-            act(lax.rem(me + i, n))
+        side, place = me // half, me % half
+
+        def across(i, carry):
+            act((1 - side) * half + lax.rem(place + i, half))
             return carry
 
-        lax.fori_loop(1, n, one, 0)
+        def along(i, carry):
+            act(side * half + lax.rem(place + i, half))
+            return carry
+
+        lax.fori_loop(0, half, across, 0)
+        lax.fori_loop(1, half, along, 0)
 
     @pl.when(step == 0)
     def _():
@@ -271,7 +278,8 @@
             pltpu.SemaphoreType.DMA((chunks + 1,)),
         ],
         compiler_params=pltpu.CompilerParams(
-            collective_id=0, has_side_effects=True, dimension_semantics=("arbitrary",)
+            collective_id=0, has_side_effects=True, dimension_semantics=("arbitrary",),
+            vmem_limit_bytes=48 * 2**20,
         ),
     )(wavenumber, coeff, values)
     return jnp.transpose(grid, (0, 2, 1))

time: 62.1 us -> 61.5 us (level)
  the two profiles are of different devices: /device:TPU:15 before, /device:TPU:0 now
where the time goes in v3:
time: 61.5 us; the launch traced here: 61.3 us
  Pallas kernels  59.4 us (97%)
  local copies, waits for them, and re-layouts  1.93 us (3%)
    pallas_call x1, Pallas kernels, on_device(): pl.pallas_call(functools.partial(transform_kernel, n, chunks, real_pairs,...  59.4 us
    unnamed x3, local copies, waits for them, and re-layouts  1.93 us

profile of v3, /device:TPU:0, one launch (start us, length us, event | category | flops | bytes accessed | tf_op | source)
XLA Modules:
  0.0 61.3 jit_solution(3460883237257577338)
XLA Ops:
  0.0 0.0 copy-start
  0.0 0.7 %copy-done = s32[80]{0:T(128)S(1)} copy-done((s32[80]{0:T(128)S(1)}, s32[80]{0:T(128)}, u32[]{:S(2)}) %copy-start) | copy-done | bytes 344
  0.7 59.4 %shard_map.37 = f32[6,32,2560]{2,1,0:T(8,128)S(1)} custom-call(s32[80]{0:T(128)S(1)} %copy-done, bf16[80,64,1280]{2,1,0:T(8,128)(2,1)} %bitcast.6, bf16[80,48,1280]{2,1,0:T(8,128)(2,1)} %bitcast.7), custom_call_target="tpu_custom_call" | custom-call | tf_op jit(solution)/shard_map/pallas_call | solution.py:251
  60.0 1.3 %copy.5 = f32[6,2560,32]{1,2,0:T(8,128)} copy(f32[6,2560,32]{1,2,0:T(8,128)S(1)} %bitcast.5) | data formatting | bytes 3932160
Async XLA Ops:
  0.0 0.7 %copy-start = (s32[80]{0:T(128)S(1)}, s32[80]{0:T(128)}, u32[]{:S(2)}) copy-start(s32[80]{0:T(128)} %wave_smem.1) | copy-start | bytes 964
